TPU v7x, 32 devices: a whole 2x2x4 slice. The times are simulated.
32 devices in a mesh: req: 8 (over z, x), seq: 4 (over y, core).
Axes of the slice: x: 2, y: 2, z: 4, core: 2. Of those that a mesh axis runs over, the one named last changes fastest.
Arguments:
- pool_states: float32 [104, 64, 64, 128], P('req', 'seq'), may hold values from -6 to 6
- inner_window: bfloat16 [104, 3, 4096], P('req', None, 'seq'), may hold values from -6 to 6
- state_window: bfloat16 [104, 3, 256], P('req', None, 'seq'), may hold values from -6 to 6
- move_plan: int32 [104, 2], P('req'), may hold values from 0 to 12, as said below
- active_mask: int32 [104], P('req'), may hold values 0 or 1
- inputs_inner: bfloat16 [8, 2048, 4096], P('req', 'seq'), may hold values from -6 to 6
- inputs_state: bfloat16 [8, 2048, 256], P('req', 'seq'), may hold values from -6 to 6
- gate_rows: bfloat16 [8, 2048, 4096], P('req', 'seq'), may hold values from -6 to 6
- step_raw: bfloat16 [8, 2048, 64], P('req', 'seq'), may hold values from -8 to 60
- lengths: int32 [8], P('req'), may hold values from 4 to 2048
- conv_weight: float32 [4, 4352], replicated, may hold values from -3 to 3
- conv_bias: float32 [4352], replicated, may hold values from -3 to 3
- step_bias: float32 [64], replicated, may hold values from -3.3 to -2.7
- decay_log: float32 [64], replicated, may hold values from -10 to 0
- skip_weight: float32 [64], replicated, may hold values from 0.5 to 1.5
- norm_weight: float32 [4096], replicated, may hold values from 0.25 to 1.75
Outputs:
- new_states: float32 [104, 64, 64, 128], P('req', 'seq')
- new_inner_window: bfloat16 [104, 3, 4096], P('req', None, 'seq')
- new_state_window: bfloat16 [104, 3, 256], P('req', None, 'seq')
- mixer_out: bfloat16 [8, 2048, 4096], P('req', 'seq')
Inputs may be any that keep to these rules, and one draw needn't show every extreme that they name: `move_plan`: every pair of a destination index along req and a slot 0 .. 12 is named exactly once; the rows of one device name one destination at most 4 times, and some destination exactly 4 times.
All inputs are finite; a program needn't handle non-finite values. No bound on the sum of `active_mask` on one device may be relied on, other than what follows from the above.
Results may differ from a plain program's by a relative error of at most 0.0087.
Values may be sent and summed in bfloat16 or wider, within the bound.
A program may use at most 192 MiB of HBM per device.

v0:
```python
import functools

import jax
import jax.numpy as jnp
from jax import lax
from jax.experimental import pallas as pl
from jax.experimental.pallas import tpu as pltpu
from jax.sharding import PartitionSpec as P

HEAD_DIM = 64
STATE_DIM = 128
KERNEL = 4
BLOCK_LEN = 256
PREFILLS = 1
INNER_DIM = 4096


EPSILON = 1e-05


def shifted(value, axis, steps):
    count = lax.axis_size(axis)
    leading, last = (max(0, -steps), min(count, count - steps))
    return lax.ppermute(value, axis, [(source, source + steps) for source in range(leading, last)])


def entering(shard, axis, combine, identity):
    peers, index = (lax.axis_size(axis), lax.axis_index(axis))
    everything = jax.tree.map(lambda part: lax.all_gather(part, axis), shard)
    start = jax.tree.map(
        lambda part, zero: jnp.broadcast_to(jnp.asarray(zero, part.dtype), part.shape),
        shard,
        identity,
    )

    def hop(k, before):
        reached = k < index
        new = combine(before, jax.tree.map(lambda part: part[k], everything))
        return jax.tree.map(lambda a, b: jnp.where(reached, a, b), new, before)

    return lax.fori_loop(0, peers, hop, start)


def conv_silu(window, new_rows, weight, bias_values):
    extended = jnp.concatenate([window, new_rows], axis=1).astype(jnp.float32)
    length = new_rows.shape[1]
    running = jnp.zeros(new_rows.shape, jnp.float32) + bias_values
    for offset in range(weight.shape[0]):
        running = running + weight[offset] * extended[:, offset : offset + length]
    return jax.nn.silu(running).astype(jnp.bfloat16)


def block_local(value_rows, write_rows, read_rows, step_rows, decay_rates):
    log_decay = step_rows * decay_rates
    running_log = jnp.cumsum(log_decay, axis=0)
    scores = lax.dot_general(
        read_rows, write_rows, (((1,), (1,)), ((), ())), preferred_element_type=jnp.float32
    )
    log_heads = running_log.T
    log_gaps = log_heads[:, :, None] - log_heads[:, None, :]
    positions = jnp.arange(running_log.shape[0])
    causal = positions[:, None] >= positions[None, :]
    decays = jnp.where(causal, jnp.exp(jnp.where(causal, log_gaps, 0.0)), 0.0)
    weights = (scores[None] * decays * step_rows.T[:, None, :]).astype(jnp.bfloat16)
    intra_part = jnp.einsum("hts,shp->thp", weights, value_rows, preferred_element_type=jnp.float32)
    to_end = jnp.exp(running_log[-1:] - running_log) * step_rows
    scaled = (to_end[:, :, None] * value_rows.astype(jnp.float32)).astype(jnp.bfloat16)
    block_state = jnp.einsum("shp,sn->hpn", scaled, write_rows, preferred_element_type=jnp.float32)
    return (intra_part, block_state, running_log)


def local_parts(value_rows, write_rows, read_rows, step_rows, decay_rates):
    batch_size = value_rows.shape[0]
    block_count = value_rows.shape[1] // BLOCK_LEN

    def to_items(source):
        return source.reshape((batch_size * block_count, BLOCK_LEN) + source.shape[2:])

    def from_items(source):
        return source.reshape((batch_size, block_count) + source.shape[1:])

    def one_item(pieces):
        return block_local(pieces[0], pieces[1], pieces[2], pieces[3], decay_rates)

    results = lax.map(
        one_item,
        (to_items(value_rows), to_items(write_rows), to_items(read_rows), to_items(step_rows)),
    )
    return tuple((from_items(result) for result in results))


def blocked(source):
    return source.reshape(
        (source.shape[0], source.shape[1] // BLOCK_LEN, BLOCK_LEN) + source.shape[2:]
    )


def fold_states(initial, block_states, running_logs):

    def fold_advance(carried, pieces):
        return (jnp.exp(pieces[1][:, -1])[:, :, None, None] * carried + pieces[0], None)

    final_state, unused = lax.scan(
        fold_advance, initial, (jnp.moveaxis(block_states, 1, 0), jnp.moveaxis(running_logs, 1, 0))
    )
    return final_state


def run_states(initial, block_states, running_logs, read_blocks):

    def run_advance(carried, pieces):
        block_state, running_log, read_block = pieces
        inter_part = (
            jnp.einsum(
                "bqn,bhpn->bqhp",
                read_block.astype(jnp.float32),
                carried,
                precision=lax.Precision.HIGHEST,
            )
            * jnp.exp(running_log)[:, :, :, None]
        )
        updated = jnp.exp(running_log[:, -1])[:, :, None, None] * carried + block_state
        return (updated, inter_part)

    final_state, inter_parts = lax.scan(
        run_advance,
        initial,
        (
            jnp.moveaxis(block_states, 1, 0),
            jnp.moveaxis(running_logs, 1, 0),
            jnp.moveaxis(read_blocks, 1, 0),
        ),
    )
    return (final_state, jnp.moveaxis(inter_parts, 0, 1))


def assemble(intra_part, inter_parts, value_rows, skip_own, valid_rows):
    combined = (intra_part + inter_parts).reshape(value_rows.shape) + skip_own[
        :, None
    ] * value_rows.astype(jnp.float32)
    combined = combined * valid_rows[:, :, None, None]
    return combined.astype(jnp.bfloat16).reshape(value_rows.shape[0], value_rows.shape[1], -1)


def gated_norm(payload_array, gate_part, norm_weight):
    gated_rows = payload_array.astype(jnp.float32) * jax.nn.silu(gate_part.astype(jnp.float32))
    norm_scale = lax.rsqrt(jnp.mean(gated_rows * gated_rows, axis=-1, keepdims=True) + EPSILON)
    return (gated_rows * norm_scale * norm_weight).astype(jnp.bfloat16)


def last_rows(raw_rows, positions):

    def pick_rows(source_rows, indices):
        return jnp.take(source_rows, indices, axis=0)

    return jax.vmap(pick_rows)(raw_rows, positions)


def pack_kernel(source_ref, keep_ref, state_ref, out_ref):
    keep = keep_ref[pl.program_id(0)].astype(jnp.float32)
    out_ref[...] = (state_ref[...] * keep).astype(out_ref.dtype)


def pack_states(states, source_slot, keep):
    count = source_slot.shape[0]
    rows, lanes = states.shape[1:]
    return pl.pallas_call(
        pack_kernel,
        grid_spec=pltpu.PrefetchScalarGridSpec(
            num_scalar_prefetch=2,
            grid=(count,),
            in_specs=[pl.BlockSpec((1, rows, lanes), lambda i, source, keep: (source[i], 0, 0))],
            out_specs=pl.BlockSpec((1, rows, lanes), lambda i, source, keep: (i, 0, 0)),
        ),
        out_shape=jax.ShapeDtypeStruct((count, rows, lanes), jnp.bfloat16),
        compiler_params=pltpu.CompilerParams(dimension_semantics=("arbitrary",)),
        cost_estimate=pl.CostEstimate(
            flops=count * rows * lanes, bytes_accessed=6 * count * rows * lanes, transcendentals=0
        ),
    )(source_slot, keep, states)


def unpack_kernel(prefills, several, first_ref, later_ref, pick_ref, *refs):
    final_ref, head_ref = refs[:2]
    out_ref = refs[-1]
    slot = pl.program_id(0)

    @pl.when(slot < prefills)
    def _():
        out_ref[...] = final_ref[...]

    @pl.when((slot >= prefills) & (pick_ref[slot] == 0))
    def _():
        out_ref[...] = head_ref[...].astype(out_ref.dtype)

    if several:

        @pl.when((slot >= prefills) & (pick_ref[slot] != 0))
        def _():
            out_ref[...] = refs[2][...].astype(out_ref.dtype)


def unpack_states(final_own, head, rest, first, later, pick, slots):
    prefills, rows, lanes = final_own.shape
    block = (1, rows, lanes)
    several = rest is not None
    operands = [final_own, head] + ([rest] if several else [])
    in_specs = [
        pl.BlockSpec(block, lambda i, f, l, p: (jnp.minimum(i, prefills - 1), 0, 0)),
        pl.BlockSpec(block, lambda i, f, l, p: (f[i], 0, 0)),
    ]
    if several:
        in_specs.append(pl.BlockSpec(block, lambda i, f, l, p: (l[i], 0, 0)))
    return pl.pallas_call(
        functools.partial(unpack_kernel, prefills, several),
        grid_spec=pltpu.PrefetchScalarGridSpec(
            num_scalar_prefetch=3,
            grid=(slots,),
            in_specs=in_specs,
            out_specs=pl.BlockSpec(block, lambda i, f, l, p: (i, 0, 0)),
        ),
        out_shape=jax.ShapeDtypeStruct((slots, rows, lanes), jnp.float32),
        compiler_params=pltpu.CompilerParams(dimension_semantics=("arbitrary",)),
        cost_estimate=pl.CostEstimate(
            flops=slots * rows * lanes, bytes_accessed=6 * slots * rows * lanes, transcendentals=0
        ),
    )(first, later, pick, *operands)


def held_forward(indices, used):
    count = indices.shape[0]
    order = jnp.arange(count, dtype=jnp.int32)
    usable = used[None, :] & (order[None, :] <= order[:, None])
    last_used = jnp.max(jnp.where(usable, order[None, :], -1), axis=1)
    match = order[None, :] == last_used[:, None]
    return jnp.sum(jnp.where(match, indices[None, :], 0), axis=1).astype(jnp.int32)


def exchange(source):
    return lax.all_to_all(source, "req", split_axis=0, concat_axis=0, tiled=True)


def ranks_of(target_device, target_slot):
    slot_count = target_slot.shape[-1]
    slot_index = jnp.arange(slot_count, dtype=jnp.int32)
    order = jnp.where(target_slot < PREFILLS, slot_index, slot_index + slot_count)
    same = target_device[..., None, :] == target_device[..., :, None]
    earlier = same & (order[..., None, :] < order[..., :, None])
    return jnp.sum(earlier.astype(jnp.int32), axis=-1)


def migrate(pool_states, inner_window, state_window, move_plan, active_mask):
    slot_count = pool_states.shape[0]
    peer_count = lax.axis_size("req")
    capacity = (2 * slot_count + peer_count - 1) // peer_count
    keep_flag = active_mask.astype(jnp.float32)
    slot_index = jnp.arange(slot_count, dtype=jnp.int32)
    send_rank = ranks_of(move_plan[:, 0], move_plan[:, 1])
    peers = jnp.arange(peer_count)
    matches = (move_plan[:, 0][None, None, :] == peers[None, :, None]) & (
        send_rank[None, None, :] == jnp.arange(capacity)[:, None, None]
    )
    source_slot = jnp.sum(jnp.where(matches, slot_index[None, None, :], 0), axis=2)
    filled = jnp.any(matches, axis=2)
    every_plan = lax.all_gather(move_plan, "req")
    every_rank = ranks_of(every_plan[..., 0], every_plan[..., 1])
    mine = every_plan[..., 0] == lax.axis_index("req")
    hits = (mine[..., None] & (every_plan[..., 1][..., None] == slot_index)).astype(jnp.int32)
    from_peer = jnp.sum(hits * peers[:, None, None], axis=(0, 1)).astype(jnp.int32)
    from_rank = jnp.sum(hits * every_rank[..., None], axis=(0, 1)).astype(jnp.int32)

    windows = jnp.concatenate([inner_window, state_window], axis=2)
    windows = (windows.astype(jnp.float32) * keep_flag[:, None, None]).astype(jnp.bfloat16)
    send_windows = jnp.take(windows, source_slot.T.reshape(-1), axis=0)
    got_windows = exchange(send_windows.reshape((peer_count, capacity) + windows.shape[1:]))
    got_windows = got_windows.reshape((-1,) + windows.shape[1:])
    moved_windows = jnp.take(got_windows, from_peer * capacity + from_rank, axis=0)

    flat_states = pool_states.reshape(slot_count, -1, pool_states.shape[-1])

    def sent(low, high):
        part, used = source_slot[low:high].T.reshape(-1), filled[low:high].T.reshape(-1)
        keep = jnp.sum(
            jnp.where(part[:, None] == slot_index[None, :], active_mask[None, :], 0), axis=1
        )
        packed = pack_states(flat_states, held_forward(part, used), keep.astype(jnp.int32))
        return packed.reshape((peer_count, high - low) + packed.shape[1:])

    head = exchange(sent(0, 1)).reshape((peer_count,) + flat_states.shape[1:])
    rest = None
    if capacity > 1:
        later_send = sent(1, capacity)
        later_send, head = lax.optimization_barrier((later_send, head))
        rest = exchange(later_send).reshape((-1,) + flat_states.shape[1:])
    in_head = from_rank == 0
    first = held_forward(from_peer, in_head)
    later = held_forward(from_peer * max(1, capacity - 1) + from_rank - 1, ~in_head)
    pick = from_rank
    initial_own = lax.dynamic_index_in_dim(head, from_peer[0], 0, keepdims=True)
    initial_own = initial_own.astype(jnp.float32).reshape((PREFILLS,) + pool_states.shape[1:])
    inner_width = inner_window.shape[2]

    def place(final_own):
        final_rows = final_own.reshape((PREFILLS,) + flat_states.shape[1:])
        placed = unpack_states(final_rows, head, rest, first, later, pick, slot_count)
        return placed.reshape(pool_states.shape)

    return (
        initial_own,
        place,
        moved_windows[:, :, :inner_width],
        moved_windows[:, :, inner_width:],
    )


def combine_carries(earlier_part, later_part):
    return (
        earlier_part[0] * later_part[0],
        later_part[1] + later_part[0][:, :, None, None] * earlier_part[1],
    )


def on_device(
    pool_states,
    inner_window,
    state_window,
    move_plan,
    active_mask,
    inputs_inner,
    inputs_state,
    gate_rows,
    step_raw,
    lengths,
    conv_weight,
    conv_bias,
    step_bias,
    decay_log,
    skip_weight,
    norm_weight,
):
    initial_own, place, moved_inner, moved_outer = migrate(
        pool_states, inner_window, state_window, move_plan, active_mask
    )
    chain_index = lax.axis_index("seq")
    chain_size = lax.axis_size("seq")
    local_length = inputs_inner.shape[1]
    local_heads = initial_own.shape[1]
    decay_rates = -jnp.exp(decay_log)
    offsets = jnp.arange(KERNEL - 1, dtype=jnp.int32)
    raw_rows = jnp.concatenate([inputs_inner, inputs_state], axis=2)
    earlier_rows = shifted(raw_rows[:, local_length - KERNEL + 1 :], "seq", 1)
    initial, head_inner, head_outer = (
        lax.all_gather(initial_own, "seq", axis=1, tiled=True),
        lax.all_gather(moved_inner[:PREFILLS].astype(jnp.float32), "seq", axis=2, tiled=True),
        lax.all_gather(moved_outer[:PREFILLS].astype(jnp.float32), "seq", axis=2, tiled=True),
    )
    first_window = jnp.concatenate([head_inner, head_outer], axis=2).astype(jnp.bfloat16)
    window = jnp.where(chain_index == 0, first_window, earlier_rows)
    mixed_rows = conv_silu(window, raw_rows, conv_weight, conv_bias)
    positions = chain_index * local_length + jnp.arange(local_length, dtype=jnp.int32)
    valid_rows = (positions[None, :] < lengths[:, None]).astype(jnp.float32)
    step_sizes = jax.nn.softplus(step_raw.astype(jnp.float32) + step_bias) * valid_rows[:, :, None]
    value_rows = mixed_rows[:, :, :INNER_DIM].reshape(PREFILLS, local_length, -1, HEAD_DIM)
    write_rows = mixed_rows[:, :, INNER_DIM : INNER_DIM + STATE_DIM]
    read_rows = mixed_rows[:, :, INNER_DIM + STATE_DIM :]
    intra_part, block_states, running_logs = local_parts(
        value_rows, write_rows, read_rows, step_sizes, decay_rates
    )
    local_end = fold_states(jnp.zeros_like(block_states[:, 0]), block_states, running_logs)
    device_decay = jnp.exp(jnp.sum(step_sizes * decay_rates, axis=1))
    every_decay = lax.all_gather(device_decay[None], "seq", axis=0, tiled=True)
    prior_decay, prior_state = entering(
        (device_decay, local_end),
        "seq",
        combine_carries,
        (jnp.ones_like(device_decay), jnp.zeros_like(local_end)),
    )
    incoming = prior_state + prior_decay[:, :, None, None] * initial
    unused_final, inter_parts = run_states(incoming, block_states, running_logs, blocked(read_rows))
    later_mask = jnp.arange(chain_size)[:, None, None] > chain_index
    suffix = jnp.prod(jnp.where(later_mask, every_decay, 1.0), axis=0)
    whole_decay = jnp.prod(every_decay, axis=0)
    window_pos = lengths[:, None] - (KERNEL - 1) + offsets[None, :] - chain_index * local_length
    inside = ((window_pos >= 0) & (window_pos < local_length)).astype(jnp.float32)
    window_term = (
        last_rows(raw_rows, jnp.clip(window_pos, 0, local_length - 1)).astype(jnp.float32)
        * inside[:, :, None]
    )
    state_sum, inner_sum, outer_sum = (
        lax.psum_scatter(
            local_end * suffix[:, :, None, None], "seq", scatter_dimension=1, tiled=True
        ),
        lax.psum_scatter(window_term[:, :, :INNER_DIM], "seq", scatter_dimension=2, tiled=True),
        lax.psum_scatter(window_term[:, :, INNER_DIM:], "seq", scatter_dimension=2, tiled=True),
    )
    own_decay = lax.dynamic_slice_in_dim(whole_decay, chain_index * local_heads, local_heads, 1)
    final_own = state_sum + own_decay[:, :, None, None] * initial_own
    kept_inner = inner_sum.astype(jnp.bfloat16)
    kept_outer = outer_sum.astype(jnp.bfloat16)
    mixer_rows = assemble(intra_part, inter_parts, value_rows, skip_weight, valid_rows)
    mixer_out = gated_norm(mixer_rows, gate_rows, norm_weight)
    new_states = place(final_own)
    new_inner = jnp.concatenate([kept_inner, moved_inner[PREFILLS:]], axis=0)
    new_outer = jnp.concatenate([kept_outer, moved_outer[PREFILLS:]], axis=0)
    return (new_states, new_inner, new_outer, mixer_out)


def solution(mesh):
    return jax.shard_map(
        on_device,
        mesh=mesh,
        in_specs=(
            P("req", "seq", None, None),
            P("req", None, "seq"),
            P("req", None, "seq"),
            P("req", None),
            P("req"),
            P("req", "seq", None),
            P("req", "seq", None),
            P("req", "seq", None),
            P("req", "seq", None),
            P("req"),
            P(),
            P(),
            P(),
            P(),
            P(),
            P(),
        ),
        out_specs=(
            P("req", "seq", None, None),
            P("req", None, "seq"),
            P("req", None, "seq"),
            P("req", "seq", None),
        ),
        check_vma=False,
    )
```

profile of v0, /device:TPU:0, one launch (start us, length us, event | category | flops | bytes accessed | tf_op | source)
XLA Modules:
  0.0 361.6 jit_solution(6218070920709365392)
XLA Ops:
  7.3 2.6 constant_dynamic-update-slice_fusion.1
  10.0 2.1 copy-done.7
  12.1 2.4 collective-permute-start
  15.2 1.6 gather_fusion.2
  20.3 6.6 %all-to-all-start = ((bf16[8,4,3,1088]{3,1,2,0:T(4,128)(2,1)}), bf16[8,4,3,1088]{3,1,2,0:T(4,128)(2,1)S(1)}, u32[]{:S(2)}, u32[]{:S(2)}) async-start(bf16[8,4,3,1088]{3,1,2,0:T(4,128)(2,1)} %copy_select_fusion), calls=%async_computation | async-start | bytes 442368 | tf_op jit(solution)/shard_map/all_to_all | solution.py:240
  27.0 3.7 %copy.136 = f32[1,3,4096]{1,0,2:T(1,128)} copy(f32[1,3,4096]{2,1,0:T(4,128)S(1)} %slice.155) | data formatting | bytes 98304
  30.8 21.0 %all-gather.3 = s32[8,13,2]{1,2,0:T(2,128)S(1)} all-gather(s32[1,13,2]{1,2,0:T(2,128)S(1)} %bitcast.283), channel_id=2, replica_groups=mesh['req'=8,'seq'=4] {'req'}, dimensions={0}, use_global_device_ids=true | all-gather | bytes 936 | tf_op jit(solution)/shard_map/all_gather | solution.py:265
  53.8 5.6 %all-reduce = f32[256]{0:T(256)S(1)} all-reduce(f32[256]{0:T(256)S(1)} %exponential_dynamic-update-slice_fusion), channel_id=3, replica_groups=mesh['req'=8,'seq'=4] {'seq'}, use_global_device_ids=true, to_apply=%add | all-reduce | flops 256 | bytes 2048
  61.6 6.4 %all_gather.29 = bf16[1,3,256]{1,0,2:T(2,128)(2,1)S(1)} all-gather(bf16[1,3,64]{1,0,2:T(2,128)(2,1)S(1)} %copy.114), channel_id=1, replica_groups=mesh['req'=8,'seq'=4] {'seq'}, dimensions={2}, use_global_device_ids=true | all-gather | bytes 1920 | tf_op jit(solution)/shard_map/all_gather | solution.py:355
  68.1 5.7 %all_gather.28 = bf16[1,3,4096]{2,1,0:T(4,128)(2,1)S(1)} all-gather(bf16[1,3,1024]{2,1,0:T(4,128)(2,1)S(1)} %slice.209), channel_id=1, replica_groups=mesh['req'=8,'seq'=4] {'seq'}, dimensions={2}, use_global_device_ids=true | all-gather | bytes 30720 | tf_op jit(solution)/shard_map/all_gather | solution.py:354
  73.8 3.2 maximum_convert_fusion
  77.0 5.7 %multiply_convert_fusion.5 = bf16[1,512,4352]{2,1,0:T(8,128)(2,1)S(1)} fusion(f32[1,515,4352]{2,1,0:T(8,128)S(1)} %maximum_convert_fusion, f32[4352]{0:T(1024)S(1)} %get-tuple-element.373, f32[4352]{0:T(1024)S(1)} %get-tuple-element.374, f32[4352]{0:T(1024)S(1)} %get-tuple-element.372, f32[4352]{0:T(1024)S(1)} %get-tuple-element.371, f32[4352]{0:T(1024)S(1)} %copy-done.13), kind=kLoop, calls=%fused_computation.75 | loop fusion | flops 28966912 | bytes 40195072 | tf_op jit(solution)/shard_map/convert_element_type | solution.py:50
  82.8 2.9 slice.152
  86.2 12.6 %reshape.688 = bf16[2,256,64,64]{3,2,1,0:T(8,128)(2,1)} reshape(bf16[1,512,4096]{2,1,0:T(8,128)(2,1)} %slice.152) | data formatting | bytes 8388608 | tf_op jit(solution)/shard_map/reshape;reshape | solution.py:77
  98.8 10.5 %copy.117 = bf16[2,256,64,64]{1,3,2,0:T(8,128)(2,1)} copy(bf16[2,256,64,64]{3,2,1,0:T(8,128)(2,1)} %reshape.688) | data formatting | bytes 8388608 | tf_op jit(solution)/shard_map/while | solution.py:85
  109.3 24.6 %while.53 = (s32[]{:T(128)}, f32[2,256,64,64]{1,3,2,0:T(8,128)}, f32[2,64,64,128]{3,2,1,0:T(8,128)}, f32[2,256,64]{1,2,0:T(8,128)S(1)}, bf16[2,256,64,64]{1,3,2,...) while((s32[]{:T(128)}, f32[2,256,64,64]{1,3,2,0:T(8,128)}, ...), condition=%wide.region_12.13_spmd, body=%wide.region_9.12_spmd.sunk | while | flops 852639936 | bytes 62990296 | solution.py:85
  110.6 7.9 %bitcast_dynamic-update-slice_fusion.8 = f32[2,256,64,64]{1,3,2,0:T(8,128)} fusion(f32[2,256,64,64]{1,3,2,0:T(8,128)} %get-tuple-element.624, s32[]{:T(128)S(6)} %copy.183, f32[64,256]{1,0:T(8,128)S(1)} %bitcast.266, f32[64,256]{1,0:T(8,128)S(1)} %get-tuple-element.592, f32[256,256]{1,0:T(8,128)S(1)} %fusion.87, ...), kind=kOutput, calls=%fused_computation.22.clone.1 | convolution fusion | flops 562036736 | bytes 6816768 | tf_op jit(solution)/shard_map/while/body/eval_jaxpr/hts,shp->thp/dot_general | solution.py:65
  119.7 1.9 copy-done.1
  122.9 7.9 %bitcast_dynamic-update-slice_fusion.8 = f32[2,256,64,64]{1,3,2,0:T(8,128)} fusion(f32[2,256,64,64]{1,3,2,0:T(8,128)} %get-tuple-element.624, s32[]{:T(128)S(6)} %copy.183, f32[64,256]{1,0:T(8,128)S(1)} %bitcast.266, f32[64,256]{1,0:T(8,128)S(1)} %get-tuple-element.592, f32[256,256]{1,0:T(8,128)S(1)} %fusion.87, ...), kind=kOutput, calls=%fused_computation.22.clone.1 | convolution fusion | flops 562036736 | bytes 6816768 | tf_op jit(solution)/shard_map/while/body/eval_jaxpr/hts,shp->thp/dot_general | solution.py:65
  132.0 1.9 copy-done.1
  134.0 3.9 %while.55 = (s32[]{:T(128)}, f32[1,64,64,128]{3,2,1,0:T(8,128)S(1)}, f32[2,1,256,64]{3,2,1,0:T(8,128)S(1)}, f32[2,1,64,64,128]{4,3,2,1,0:T(8,128)}, s32[]{:T(128)}, /*index=5*/s32[]{:T(128)}) while((s32[]{:T(128)}, f32[1,64,64,128]{3,2,1,0:T(8,128)S(1)}, f32[2,1,256,64]{3,2,1,0:T(8,128)S(1)}, f32[2,1,64,64,128]{4,3,2,1,0:T(8,128)}, ...), condition=%wide.region_14.15_spmd.clone, body=%wide.region_13.14_spmd.clone.sunk | while | flops 1572867 | bytes 6423391 | solution.py:103
  134.1 1.9 bitcast_add_fusion.8
  136.1 1.9 bitcast_add_fusion.8
  138.0 1.7 broadcast_multiply_fusion
  142.0 6.4 %shard_map.184 = bf16[8,1024,128]{2,1,0:T(8,128)(2,1)} custom-call(s32[8]{0:T(128)} %select_reduce_fusion.10.source_ref, s32[8]{0:T(128)} %select_reduce_fusion.9.keep_ref, f32[13,1024,128]{2,1,0:T(8,128)} %bitcast.250), custom_call_target="tpu_custom_call" | custom-call | flops 1048576 | bytes 6291456 | tf_op jit(solution)/shard_map/pallas_call | solution.py:167
  148.4 3.6 all-to-all-start.1
  153.8 14.3 %shard_map.183 = bf16[24,1024,128]{2,1,0:T(8,128)(2,1)} custom-call(s32[24]{0:T(128)} %select_reduce_fusion.2.source_ref, s32[24]{0:T(128)} %select_reduce_fusion.4.keep_ref, f32[13,1024,128]{2,1,0:T(8,128)} %bitcast.251), custom_call_target="tpu_custom_call" | custom-call | flops 3145728 | bytes 18874368 | tf_op jit(solution)/shard_map/pallas_call | solution.py:167
  168.1 32.8 %all-to-all-done.1 = bf16[8,1,1024,128]{3,2,1,0:T(8,128)(2,1)S(1)} async-done(((bf16[8,1,1024,128]{3,2,1,0:T(8,128)(2,1)}), bf16[8,1,1024,128]{3,2,1,0:T(8,128)(2,1)S(1)}, u32[]{:S(2)}, u32[]{:S(2)}) %all-to-all-start.1) | async-done | bytes 2097184 | tf_op jit(solution)/shard_map/all_to_all | solution.py:240
  202.2 4.8 %all-to-all-start.2 = ((bf16[8,3,1024,128]{3,2,1,0:T(8,128)(2,1)}), bf16[8,3,1024,128]{3,2,1,0:T(8,128)(2,1)}, u32[]{:S(2)}, u32[]{:S(2)}) async-start(bf16[8,3,1024,128]{3,2,1,0:T(8,128)(2,1)} %bitcast.252), calls=%async_computation.3 | async-start | bytes 12582912 | tf_op jit(solution)/shard_map/all_to_all | solution.py:240
  214.8 2.0 fusion.46
  216.7 11.2 %all-gather.9.cloned.1.call-done = f32[4,64,64,128]{3,2,1,0:T(8,128)} async-done(((f32[1,64,64,128]{3,2,1,0:T(8,128)}), f32[4,64,64,128]{3,2,1,0:T(8,128)}) %all-gather.9.cloned.1.call-update) | async-done | bytes 8388624 | tf_op jit(solution)/shard_map/all_gather | solution.py:29
  227.9 8.7 %while.56 = (s32[]{:T(128)}, f32[1,64]{1,0:T(1,128)S(1)}, f32[1,64,64,128]{3,2,1,0:T(8,128)S(1)}, s32[]{:T(128)}, f32[4,1,64]{2,1,0:T(1,128)S(1)}, /*index=5*/f32[4,1,64,64,128]{4,3,2,1,0:T(8,128)}, s32[]{:T(128)}, s32[]{:T(128)}) while((s32[]{:T(128)}, f32[1,64]{1,0:T(1,128)S(1)}, f32[1,64,64,128]{3,2,1,0:T(8,128)S(1)}, ...), condition=%wide.region_29.30_spmd.clone, body=%wide.region_28.29_spmd.clone.sunk | while | flops 2097348 | bytes 6293119 | solution.py:41
  227.9 2.1 fusion.93
  230.1 2.1 fusion.93
  232.2 2.1 fusion.93
  234.4 2.2 fusion.93
  236.6 15.3 %all-gather.7.cloned.1.call-done = f32[1,64,64,128]{3,2,0,1:T(8,128)} async-done(((f32[1,16,64,128]{3,2,0,1:T(8,128)}), f32[1,64,64,128]{3,2,0,1:T(8,128)}) %all-gather.7.cloned.1.call-update) | async-done | bytes 2097168 | tf_op jit(solution)/shard_map/all_gather | solution.py:353
  251.9 2.5 fusion.45
  254.4 8.9 %while.54 = (s32[]{:T(128)}, f32[1,64,64,128]{3,2,1,0:T(8,128)S(1)}, f32[2,1,256,64,64]{2,4,3,1,0:T(8,128)}, f32[2,1,256,64]{2,3,1,0:T(8,128)S(1)}, f32[2,1,64,6...) while((s32[]{:T(128)}, f32[1,64,64,128]{3,2,1,0:T(8,128)S(1)}, ...), condition=%wide.region_31.32_spmd, body=%wide.region_30.31_spmd.sunk | while | flops 1612709888 | bytes 29689720 | solution.py:125
  254.5 3.7 %bitcast_dynamic-update-slice_fusion.11 = f32[2,1,256,64,64]{2,4,3,1,0:T(8,128)} fusion(f32[2,1,256,64,64]{2,4,3,1,0:T(8,128)} %get-tuple-element.696, s32[]{:T(128)S(6)} %copy.210, f32[1,64,64,128]{3,2,1,0:T(8,128)S(1)} %get-tuple-element.695, f32[256,64]{0,1:T(8,128)S(1)} %get-tuple-element.601, bf16[2,1,256,128]{3,2,1,0:T(8,128)(2,1)S(1)} %get-tuple-element.706), kind=kOutput, calls=%fused_computation.55.clone.1 | convolution fusion | flops 1611661312 | bytes 6423552 | tf_op jit(solution)/shard_map/while/body/eval_jaxpr/bqn,bhpn->bqhp/dot_general | solution.py:114
  258.9 3.8 %bitcast_dynamic-update-slice_fusion.11 = f32[2,1,256,64,64]{2,4,3,1,0:T(8,128)} fusion(f32[2,1,256,64,64]{2,4,3,1,0:T(8,128)} %get-tuple-element.696, s32[]{:T(128)S(6)} %copy.210, f32[1,64,64,128]{3,2,1,0:T(8,128)S(1)} %get-tuple-element.695, f32[256,64]{0,1:T(8,128)S(1)} %get-tuple-element.601, bf16[2,1,256,128]{3,2,1,0:T(8,128)(2,1)S(1)} %get-tuple-element.706), kind=kOutput, calls=%fused_computation.55.clone.1 | convolution fusion | flops 1611661312 | bytes 6423552 | tf_op jit(solution)/shard_map/while/body/eval_jaxpr/bqn,bhpn->bqhp/dot_general | solution.py:114
  263.3 11.7 %bitcast_add_fusion.3 = f32[2,256,64,64]{1,3,2,0:T(8,128)} fusion(f32[2,256,64,64]{1,3,2,0:T(8,128)} %get-tuple-element.224, f32[2,1,256,64,64]{2,4,3,1,0:T(8,128)} %get-tuple-element.227), kind=kLoop, calls=%fused_computation.80 | loop fusion | flops 2097152 | bytes 25165824 | tf_op jit(solution)/shard_map/add | solution.py:138
  275.0 16.3 %copy.135 = f32[2,256,64,64]{3,2,1,0:T(8,128)} copy(f32[2,256,64,64]{1,3,2,0:T(8,128)} %bitcast_add_fusion.3) | data formatting | bytes 16777216 | tf_op jit(solution)/shard_map/reshape | solution.py:138
  291.3 14.8 %reshape.689 = f32[1,512,4096]{2,1,0:T(8,128)} reshape(f32[2,256,64,64]{3,2,1,0:T(8,128)} %copy.135) | data formatting | bytes 16777216 | tf_op jit(solution)/shard_map/reshape | solution.py:138
  306.0 8.5 %multiply_reduce_fusion = (f32[512]{0:T(512)S(1)}, f32[1,512,4096]{2,1,0:T(8,128)S(1)}) fusion(bf16[1,512,4096]{2,1,0:T(8,128)(2,1)} %param.31, f32[512]{0:T(512)S(1)} %copy-done.15, f32[1,512,4096]{2,1,0:T(8,128)} %reshape.689, bf16[1,512,4352]{2,1,0:T(8,128)(2,1)} %copy-done.6, f32[4096]{0:T(1024)S(1)} %mul.342), kind=kLoop, calls=%fused_computation.82 | loop fusion | flops 29359616 | bytes 25186304 | tf_op jit(solution)/shard_map/reduce_sum | solution.py:147
  314.5 3.5 multiply_convert_fusion.6
  318.0 27.1 %all-to-all-done.2 = bf16[8,3,1024,128]{3,2,1,0:T(8,128)(2,1)} async-done(((bf16[8,3,1024,128]{3,2,1,0:T(8,128)(2,1)}), bf16[8,3,1024,128]{3,2,1,0:T(8,128)(2,1)}, u32[]{:S(2)}, u32[]{:S(2)}) %all-to-all-start.2) | async-done | bytes 6291488 | tf_op jit(solution)/shard_map/all_to_all | solution.py:240
  345.0 10.0 %shard_map.185 = f32[13,1024,128]{2,1,0:T(8,128)} custom-call(s32[13]{0:T(128)} %select_reduce_fusion.7.first_ref, s32[13]{0:T(128)} %select_reduce_fusion.5.later_ref, s32[13]{0:T(128)} %copy-done.18, f32[1,1024,128]{2,1,0:T(8,128)} %bitcast.265, bf16[8,1024,128]{2,1,0:T(8,128)(2,1)} %bitcast.255, bf16[24,1024,128]{2,1,0:T(8,128)(2,1)} %bitcast.52.refs_2_), custom_call_target="tpu_custom_call" | custom-call | flops 1703936 | bytes 10223616 | tf_op jit(solution)/shard_map/pallas_call | solution.py:214
  (220 shorter events, 26.8 us)
Async XLA Ops:
  7.2 2.7 copy-start.9
  7.2 10.5 %copy-start.19 = (s32[13,2]{0,1:T(2,128)S(1)}, s32[13,2]{0,1:T(2,128)}, u32[]{:S(2)}) copy-start(s32[13,2]{0,1:T(2,128)} %param.27) | copy-start | bytes 316
  7.2 10.5 %copy-start.17 = (bf16[13,3,64]{2,0,1:T(8,128)(2,1)S(1)}, bf16[13,3,64]{2,0,1:T(8,128)(2,1)}, u32[]{:S(2)}) copy-start(bf16[13,3,64]{2,0,1:T(8,128)(2,1)} %param.26) | copy-start | bytes 14980
  7.2 10.5 %copy-start.10 = (bf16[13,3,1024]{2,0,1:T(8,128)(2,1)S(1)}, bf16[13,3,1024]{2,0,1:T(8,128)(2,1)}, u32[]{:S(2)}) copy-start(bf16[13,3,1024]{2,0,1:T(8,128)(2,1)} %param.25) | copy-start | bytes 239620
  7.2 10.6 %copy-start.23 = (s32[13]{0:T(128)S(1)}, s32[13]{0:T(128)}, u32[]{:S(2)}) copy-start(s32[13]{0:T(128)} %param.28) | copy-start | bytes 160
  7.2 202.1 %reduce-scatter.12.cloned.1.call-start = ((), (), s32[]{:S(2)}) async-start(), calls=%async_computation.10 | async-start | bytes 163840
  9.9 42.2 %copy-start.22 = (f32[64]{0:T(128)S(1)}, f32[64]{0:T(128)}, u32[]{:S(2)}) copy-start(f32[64]{0:T(128)} %param.37) | copy-start | bytes 772
  9.9 42.3 %copy-start.24 = (u32[32]{0:T(128)S(1)}, u32[32]{0:T(128)}, u32[]{:S(2)}) copy-start(u32[32]{0:T(128)} %constant.201) | copy-start | bytes 388
  9.9 43.5 %copy-start.12 = (bf16[1,512,64]{1,2,0:T(8,128)(2,1)S(1)}, bf16[1,512,64]{1,2,0:T(8,128)(2,1)}, u32[]{:S(2)}) copy-start(bf16[1,512,64]{1,2,0:T(8,128)(2,1)} %param.32) | copy-start | bytes 196612
  9.9 43.5 %copy-start.20 = (f32[64]{0:T(128)S(1)}, f32[64]{0:T(128)}, u32[]{:S(2)}) copy-start(f32[64]{0:T(128)} %param.36) | copy-start | bytes 772
  9.9 50.4 %copy-start.11 = (f32[4,4352]{1,0:T(4,128)S(1)}, f32[4,4352]{1,0:T(4,128)}, u32[]{:S(2)}) copy-start(f32[4,4352]{1,0:T(4,128)} %param.34) | copy-start | bytes 208900
  10.0 2.1 copy-start.7
  12.1 61.7 %collective-permute-start = (bf16[1,3,4352]{2,1,0:T(4,128)(2,1)S(1)}, bf16[1,3,4352]{2,1,0:T(4,128)(2,1)S(1)}, u32[]{:S(2)}, u32[]{:S(2)}) collective-permute-start(bf16[1,3,4352]{2,1,0:T(4,128)(2,1)S(1)} %slice.147), channel_id=1, source_target_pairs={{0,1},{1,2},{2,3},{4,5},{5,6},{6,7},{8,9},{9,10},{10,11},{12,13},{... | collective-permute-start | bytes 78344 | tf_op jit(solution)/shard_map/ppermute | solution.py:24
  20.3 40.2 %all-to-all-start = ((bf16[8,4,3,1088]{3,1,2,0:T(4,128)(2,1)}), bf16[8,4,3,1088]{3,1,2,0:T(4,128)(2,1)S(1)}, u32[]{:S(2)}, u32[]{:S(2)}) async-start(bf16[8,4,3,1088]{3,1,2,0:T(4,128)(2,1)} %copy_select_fusion), calls=%async_computation | async-start | bytes 442368 | tf_op jit(solution)/shard_map/all_to_all | solution.py:240
  26.9 183.2 %reduce-scatter.10.cloned.1.call-start = ((), (), s32[]{:S(2)}) async-start(), calls=%async_computation.9 | async-start | bytes 2621440
  30.7 184.1 %reduce-scatter.8.cloned.1.call-start = ((), (), s32[]{:S(2)}) async-start(), calls=%async_computation.6 | async-start | bytes 2621440 | tf_op jit(solution)/shard_map/reduce_scatter | solution.py:390
  52.1 1.7 copy-start.14
  60.0 148.5 %copy-start.18 = (s32[13]{0:T(128)}, s32[13]{0:T(128)S(1)}, u32[]{:S(2)}) copy-start(s32[13]{0:T(128)S(1)} %get-tuple-element.375.pick_ref) | copy-start | bytes 160
  73.8 3.2 copy-start.13
  82.8 3.4 copy-start.6
  110.6 8.3 %copy-start = (f32[2,64,64,128]{3,2,1,0:T(8,128)S(1)}, f32[2,64,64,128]{3,2,1,0:T(8,128)}, u32[]{:S(2)}) copy-start(f32[2,64,64,128]{3,2,1,0:T(8,128)} %get-tuple-element.625) | copy-start | bytes 12582916 | tf_op jit(solution)/shard_map/while
  110.6 8.3 %copy-start.5 = (bf16[2,256,64,64]{1,3,2,0:T(8,128)(2,1)S(1)}, bf16[2,256,64,64]{1,3,2,0:T(8,128)(2,1)}, u32[]{:S(2)}) copy-start(bf16[2,256,64,64]{1,3,2,0:T(8,128)(2,1)} %get-tuple-element.638) | copy-start | bytes 12582916 | tf_op jit(solution)/shard_map/while
  119.6 2.0 copy-start.1
  122.9 8.3 %copy-start = (f32[2,64,64,128]{3,2,1,0:T(8,128)S(1)}, f32[2,64,64,128]{3,2,1,0:T(8,128)}, u32[]{:S(2)}) copy-start(f32[2,64,64,128]{3,2,1,0:T(8,128)} %get-tuple-element.625) | copy-start | bytes 12582916 | tf_op jit(solution)/shard_map/while
  122.9 8.3 %copy-start.5 = (bf16[2,256,64,64]{1,3,2,0:T(8,128)(2,1)S(1)}, bf16[2,256,64,64]{1,3,2,0:T(8,128)(2,1)}, u32[]{:S(2)}) copy-start(bf16[2,256,64,64]{1,3,2,0:T(8,128)(2,1)} %get-tuple-element.638) | copy-start | bytes 12582916 | tf_op jit(solution)/shard_map/while
  131.9 2.0 copy-start.1
  138.0 2.1 copy-start.3
  139.7 88.2 %all-gather.9.cloned.1.call-start = ((), (), s32[]{:S(2)}) async-start(), calls=%async_computation.8 | async-start | bytes 10485760 | tf_op jit(solution)/shard_map/all_gather | solution.py:29
  148.4 52.5 %all-to-all-start.1 = ((bf16[8,1,1024,128]{3,2,1,0:T(8,128)(2,1)}), bf16[8,1,1024,128]{3,2,1,0:T(8,128)(2,1)S(1)}, u32[]{:S(2)}, u32[]{:S(2)}) async-start(bf16[8,1,1024,128]{3,2,1,0:T(8,128)(2,1)} %bitcast.256), calls=%async_computation.2 | async-start | bytes 4194304 | tf_op jit(solution)/shard_map/all_to_all | solution.py:240
  200.9 1.3 copy-start.8
  200.9 6.4 %copy-start.21 = (f32[64]{0:T(128)S(1)}, f32[64]{0:T(128)}, u32[]{:S(2)}) copy-start(f32[64]{0:T(128)} %param.38) | copy-start | bytes 772
  202.2 142.8 %all-to-all-start.2 = ((bf16[8,3,1024,128]{3,2,1,0:T(8,128)(2,1)}), bf16[8,3,1024,128]{3,2,1,0:T(8,128)(2,1)}, u32[]{:S(2)}, u32[]{:S(2)}) async-start(bf16[8,3,1024,128]{3,2,1,0:T(8,128)(2,1)} %bitcast.252), calls=%async_computation.3 | async-start | bytes 12582912 | tf_op jit(solution)/shard_map/all_to_all | solution.py:240
  207.0 44.9 %all-gather.7.cloned.1.call-start = ((), (), s32[]{:S(2)}) async-start(), calls=%async_computation.7 | async-start | bytes 2621440 | tf_op jit(solution)/shard_map/all_gather | solution.py:353
  236.6 15.3 %copy-start.4 = (f32[1,64,64,128]{3,2,1,0:T(8,128)}, f32[1,64,64,128]{3,2,1,0:T(8,128)S(1)}, u32[]{:S(2)}) copy-start(f32[1,64,64,128]{3,2,1,0:T(8,128)S(1)} %get-tuple-element.225) | copy-start | bytes 6291460
  254.4 4.0 %copy-start.2 = (f32[2,1,64,64,128]{4,3,2,1,0:T(8,128)S(1)}, f32[2,1,64,64,128]{4,3,2,1,0:T(8,128)}, u32[]{:S(2)}) copy-start(f32[2,1,64,64,128]{4,3,2,1,0:T(8,128)} %get-tuple-element.705) | copy-start | bytes 12582916 | tf_op jit(solution)/shard_map/while
  258.9 4.0 %copy-start.2 = (f32[2,1,64,64,128]{4,3,2,1,0:T(8,128)S(1)}, f32[2,1,64,64,128]{4,3,2,1,0:T(8,128)}, u32[]{:S(2)}) copy-start(f32[2,1,64,64,128]{4,3,2,1,0:T(8,128)} %get-tuple-element.705) | copy-start | bytes 12582916 | tf_op jit(solution)/shard_map/while
  291.3 14.8 %copy-start.15 = (f32[512]{0:T(512)S(1)}, f32[512]{0:T(512)}, u32[]{:S(2)}) copy-start(f32[512]{0:T(512)} %copy-done.14) | copy-start | bytes 6148
  306.0 8.5 %copy-start.16 = (f32[4096]{0:T(1024)S(1)}, f32[4096]{0:T(1024)}, u32[]{:S(2)}) copy-start(f32[4096]{0:T(1024)} %param.39) | copy-start | bytes 49156
Sparse Core Ops, SparseCore 0:
  17.8 22.2 reduce-scatter.11
  42.7 32.0 reduce-scatter.9
  139.9 28.3 reduce-scatter.7
  169.6 58.2 all-gather.8
  229.3 22.5 all-gather.6
where the time goes:
time: 364 us; the launch traced here: 362 us
  waiting for transfers between devices  86.7 us (24%)
  local copies, waits for them, and re-layouts  83.9 us (23%)
  other arithmetic  62.1 us (17%)
  blocking collectives  38.7 us (11%)
  Pallas kernels  30.7 us (8%)
  matrix products  25.2 us (7%)
  starting transfers between devices  17.8 us (5%)
  between operations  15.9 us (4%)
    all_to_all x3, waiting for transfers between devices, exchange(): lax.all_to_all(source, 'req', split_axis=0, concat_axis=0, tiled=True)  59.8 us
    reshape x2, local copies, waits for them, and re-layouts, assemble(): (intra_part + inter_parts).reshape(value_rows.shape)  31 us
    all_gather x1, blocking collectives, migrate(): every_plan = lax.all_gather(move_plan, 'req')  21 us
    pallas_call x2, Pallas kernels, pack_states(): pl.pallas_call(pack_kernel, grid_spec=pltpu.PrefetchScalarGridSpec(num_sc...  20.7 us
    dot_general x2, matrix products, block_local(): jnp.einsum('hts,shp->thp', weights, value_rows, preferred_element_type=jn...  15.9 us
    unnamed x54, local copies, waits for them, and re-layouts  15.4 us
    all_gather x1, waiting for transfers between devices, on_device(): lax.all_gather(initial_own, 'seq', axis=1, tiled=True)  15.3 us
    all_to_all x3, starting transfers between devices, exchange(): lax.all_to_all(source, 'req', split_axis=0, concat_axis=0, tiled=True)  15 us
  transfers between devices with their start and end apart: 9, of which 4 were waited for; matrix products, arithmetic and copies ran while one was open for 44% of the time, Pallas kernels for 6%

commit v1 on v0

v1 whole, which is shorter than its diff:
```python
import functools

import jax
import jax.numpy as jnp
from jax import lax
from jax.experimental import pallas as pl
from jax.experimental.pallas import tpu as pltpu
from jax.sharding import PartitionSpec as P

HEAD_DIM = 64
STATE_DIM = 128
KERNEL = 4
BLOCK_LEN = 256
EPSILON = 1e-05
LANES = 128
HALO = 8
LOG2E = 1.4426950408889634
GROUP = 2 * LANES


def half_silu(v):
    return (0.5 * v) * (1.0 + jnp.tanh(0.5 * v))


def conv_rows(ext_ref, weight_ref, bias_ref, start, count):
    total = bias_ref[...] + weight_ref[KERNEL - 1 : KERNEL, :] * ext_ref[pl.ds(start + HALO, count), :]
    for k in range(KERNEL - 1):
        total = total + weight_ref[k : k + 1, :] * ext_ref[pl.ds(start + HALO - KERNEL + 1 + k, count), :]
    return half_silu(total).astype(jnp.bfloat16)


def mix_kernel(
    nv_ref, x_ref, win_ref, cw_ref, cb_ref, skip_ref, xs_ref, wins_ref, cws_ref, cbs_ref, step_ref, sbias_ref, dlog_ref,
    part_ref, end_ref, ecum_ref, read_ref,
    ext, val, a_s, te_s, brow, write_t, score,
):
    g = pl.program_id(0)
    length = x_ref.shape[0]
    blocks = length // BLOCK_LEN
    half = BLOCK_LEN // 2

    @pl.when(g == 0)
    def _():
        ext[0:HALO, :] = wins_ref[...].astype(jnp.float32)
        ext[HALO : HALO + length, :] = xs_ref[...].astype(jnp.float32)
        ys = conv_rows(ext, cws_ref, cbs_ref, 0, length)
        write, read = ys[:, :STATE_DIM], ys[:, STATE_DIM:]
        read_ref[...] = read
        write_t[...] = write.astype(jnp.float32).T.astype(jnp.bfloat16)
        rows = lax.broadcasted_iota(jnp.int32, (length, LANES), 0)
        raw = step_ref[...] + sbias_ref[...]
        soft = jnp.maximum(raw, 0.0) + jnp.log1p(jnp.exp(-jnp.abs(raw)))
        dt = jnp.where(rows < nv_ref[0], soft, 0.0)
        rate = (dt * LOG2E) * (-jnp.exp(dlog_ref[...]))
        r = lax.broadcasted_iota(jnp.int32, (BLOCK_LEN, BLOCK_LEN), 0)
        c = lax.broadcasted_iota(jnp.int32, (BLOCK_LEN, BLOCK_LEN), 1)
        tri = (r >= c).astype(jnp.float32)
        before = jnp.zeros((1, LANES), jnp.float32)
        for blk in range(blocks):
            s = slice(blk * BLOCK_LEN, (blk + 1) * BLOCK_LEN)
            cum = jnp.dot(tri, rate[s], precision=lax.Precision.HIGHEST, preferred_element_type=jnp.float32)
            b = jnp.where(dt[s] > 0.0, cum - jnp.log2(dt[s]), 1e30)
            a_s[s, :] = cum
            last = cum[BLOCK_LEN - 1 : BLOCK_LEN, :]
            te_s[s, :] = jnp.exp2(last - b)
            brow[:, s] = b.T
            ecum_ref[s, :] = jnp.exp2(cum + before)
            before = before + last
            sc = lax.dot_general(read[s], write[s], (((1,), (1,)), ((), ())), preferred_element_type=jnp.float32)
            score[blk] = jnp.where(r >= c, sc, 0.0)

    ext[0:HALO, :] = win_ref[...].astype(jnp.float32)
    ext[HALO : HALO + length, :] = x_ref[...].astype(jnp.float32)
    rows_at_once = 64
    for i in range(length // rows_at_once):
        val[i * rows_at_once : (i + 1) * rows_at_once, :] = conv_rows(ext, cw_ref, cb_ref, i * rows_at_once, rows_at_once)

    heads_step = GROUP // HEAD_DIM
    turn = lax.rem(LANES - heads_step * g, LANES)
    a_all = pltpu.roll(a_s[...], turn, axis=1)
    te_all = pltpu.roll(te_s[...], turn, axis=1)
    low = lax.broadcasted_iota(jnp.int32, (1, LANES), 1) < HEAD_DIM

    for pair in range(GROUP // LANES):
        cols = slice(pair * LANES, (pair + 1) * LANES)
        skip = skip_ref[:, cols]
        before = None
        for blk in range(blocks):
            s = slice(blk * BLOCK_LEN, (blk + 1) * BLOCK_LEN)
            v = val[s, cols]
            vf = v.astype(jnp.float32)
            masked = [jnp.where(low, vf, 0.0).astype(jnp.bfloat16), jnp.where(low, 0.0, vf).astype(jnp.bfloat16)]
            tops, bottoms = [], []
            for j in range(2):
                h = 2 * pair + j
                a = a_all[s, h : h + 1]
                b = brow[pl.ds(heads_step * g + h, 1), s]
                top = jnp.exp2(jnp.minimum(a[:half] - b[:, :half], 126.0)) * score[blk, :half, :half]
                bot = jnp.exp2(jnp.minimum(a[half:] - b, 126.0)) * score[blk, half:, :]
                tops.append(top.astype(jnp.bfloat16))
                bottoms.append(bot.astype(jnp.bfloat16))
            intra_top = jnp.dot(
                jnp.concatenate(tops, axis=1), jnp.concatenate([m[:half] for m in masked], axis=0), preferred_element_type=jnp.float32
            )
            intra_bot = jnp.dot(
                jnp.concatenate(bottoms, axis=1), jnp.concatenate(masked, axis=0), preferred_element_type=jnp.float32
            )
            out = jnp.concatenate([intra_top, intra_bot], axis=0) + skip * vf
            h = 2 * pair
            te = jnp.where(low, te_all[s, h : h + 1], te_all[s, h + 1 : h + 2])
            state = jnp.dot(write_t[:, s], (te * vf).astype(jnp.bfloat16), preferred_element_type=jnp.float32)
            if blk > 0:
                e = jnp.exp2(jnp.where(low, a_all[s, h : h + 1], a_all[s, h + 1 : h + 2]))
                out = out + e * jnp.dot(read_ref[s, :], before.astype(jnp.bfloat16), preferred_element_type=jnp.float32)
                state = state + e[BLOCK_LEN - 1 : BLOCK_LEN, :] * before
            before = state
            part_ref[s, cols] = out.astype(jnp.bfloat16)
        end_ref[:, cols] = before.astype(jnp.bfloat16)


def mix(nv, x, xs, window, conv_weight, conv_bias, step_raw, step_bias, decay_log, skip_row):
    length, inner = x.shape
    pad = LANES - step_raw.shape[1]
    step = jnp.pad(step_raw.astype(jnp.float32), ((0, 0), (0, pad)))
    sbias = jnp.pad(step_bias, (0, pad))[None]
    dlog = jnp.pad(decay_log, (0, pad))[None]
    xs_width = xs.shape[1]
    fixed = lambda shape: pl.BlockSpec(shape, lambda i, nv: (0,) * len(shape))
    column = lambda rows: pl.BlockSpec((rows, GROUP), lambda i, nv: (0, i))
    blocks = length // BLOCK_LEN
    heads = inner // HEAD_DIM
    return pl.pallas_call(
        mix_kernel,
        grid_spec=pltpu.PrefetchScalarGridSpec(
            num_scalar_prefetch=1,
            grid=(inner // GROUP,),
            in_specs=[
                column(length), column(HALO), column(KERNEL), column(1), column(1),
                fixed((length, xs_width)), fixed((HALO, xs_width)), fixed((KERNEL, xs_width)), fixed((1, xs_width)),
                fixed((length, LANES)), fixed((1, LANES)), fixed((1, LANES)),
            ],
            out_specs=[column(length), column(STATE_DIM), fixed((length, LANES)), fixed((length, STATE_DIM))],
            scratch_shapes=[
                pltpu.VMEM((length + HALO, GROUP), jnp.float32),
                pltpu.VMEM((length, GROUP), jnp.bfloat16),
                pltpu.VMEM((length, LANES), jnp.float32),
                pltpu.VMEM((length, LANES), jnp.float32),
                pltpu.VMEM((LANES, length), jnp.float32),
                pltpu.VMEM((STATE_DIM, length), jnp.bfloat16),
                pltpu.VMEM((blocks, BLOCK_LEN, BLOCK_LEN), jnp.float32),
            ],
        ),
        out_shape=[
            jax.ShapeDtypeStruct((length, inner), jnp.bfloat16),
            jax.ShapeDtypeStruct((STATE_DIM, inner), jnp.bfloat16),
            jax.ShapeDtypeStruct((length, LANES), jnp.float32),
            jax.ShapeDtypeStruct((length, STATE_DIM), jnp.bfloat16),
        ],
        compiler_params=pltpu.CompilerParams(dimension_semantics=("arbitrary",)),
        cost_estimate=pl.CostEstimate(
            flops=2 * blocks * heads * BLOCK_LEN * BLOCK_LEN * LANES * 8,
            bytes_accessed=4 * length * inner, transcendentals=blocks * heads * BLOCK_LEN * BLOCK_LEN,
        ),
        name="mix",
    )(
        nv, x, window[:, :inner], conv_weight[:, :inner], conv_bias[None, :inner], skip_row,
        xs, window[:, inner:], conv_weight[:, inner:], conv_bias[None, inner:], step, sbias, dlog,
    )


CHUNK = 256


def finish_kernel(
    nv_ref, part_ref, gate_ref, read_ref, ecum_ref, ends_ref, coef_ref, init_ref, norm_ref, out_ref, prior, spread, gated
):
    step = pl.program_id(0)
    tile, inner = part_ref.shape
    chain = ends_ref.shape[0]
    heads = inner // HEAD_DIM

    @pl.when(step == 0)
    def _():
        def fill(i, carry):
            cols = pl.ds(pl.multiple_of(i * CHUNK, CHUNK), CHUNK)
            total = coef_ref[0:1, cols] * ends_ref[0, :, cols].astype(jnp.float32)
            for j in range(1, chain):
                total = total + coef_ref[j : j + 1, cols] * ends_ref[j, :, cols].astype(jnp.float32)
            prior[:, cols] = total.astype(jnp.bfloat16)
            k = lax.broadcasted_iota(jnp.int32, (LANES, CHUNK), 0)
            c = lax.broadcasted_iota(jnp.int32, (LANES, CHUNK), 1)
            owner = i * (CHUNK // HEAD_DIM) + c // HEAD_DIM
            spread[:, cols] = jnp.where((k == owner) | (k == owner + heads), 1.0, 0.0).astype(jnp.bfloat16)
            return carry

        lax.fori_loop(0, inner // CHUNK, fill, 0)

    read = read_ref[...]
    ecum = ecum_ref[...]
    first = ecum.astype(jnp.bfloat16).astype(jnp.float32)
    lane = lax.broadcasted_iota(jnp.int32, (tile, LANES), 1)
    both = jnp.where(lane < heads, first, pltpu.roll(ecum - first, heads, axis=1)).astype(jnp.bfloat16)
    rows = lax.broadcasted_iota(jnp.int32, (tile, 1), 0) + step * tile
    valid = (rows < nv_ref[0]).astype(jnp.float32)

    def gate_chunk(i, squares):
        cols = pl.ds(pl.multiple_of(i * CHUNK, CHUNK), CHUNK)
        z = jnp.dot(read, prior[:, cols], preferred_element_type=jnp.float32)
        zi = lax.dot_general(read, init_ref[cols, :], (((1,), (1,)), ((), ())), preferred_element_type=jnp.float32)
        e = jnp.dot(both, spread[:, cols], preferred_element_type=jnp.float32)
        z = z + coef_ref[chain : chain + 1, cols] * zi
        y = (part_ref[:, cols].astype(jnp.float32) + e * z) * valid
        y = y.astype(jnp.bfloat16).astype(jnp.float32)
        out = y * half_silu(gate_ref[:, cols].astype(jnp.float32))
        gated[:, cols] = out
        square = out * out
        for k in range(CHUNK // LANES):
            squares = squares + square[:, k * LANES : (k + 1) * LANES]
        return squares

    squares = lax.fori_loop(0, inner // CHUNK, gate_chunk, jnp.zeros((tile, LANES), jnp.float32))
    scale = lax.rsqrt(jnp.sum(squares, axis=1, keepdims=True) * (1.0 / inner) + EPSILON)

    def scale_chunk(i, carry):
        cols = pl.ds(pl.multiple_of(i * CHUNK, CHUNK), CHUNK)
        out_ref[:, cols] = (gated[:, cols] * scale * norm_ref[:, cols]).astype(jnp.bfloat16)
        return carry

    lax.fori_loop(0, inner // CHUNK, scale_chunk, 0)


def finish(nv, part, gate, read, ecum, ends, coef, initial, norm):
    length, inner = part.shape
    tile = min(128, length)
    chain = ends.shape[0]
    fixed = lambda shape: pl.BlockSpec(shape, lambda i, nv: (0,) * len(shape))
    row = lambda width: pl.BlockSpec((tile, width), lambda i, nv: (i, 0))
    return pl.pallas_call(
        finish_kernel,
        grid_spec=pltpu.PrefetchScalarGridSpec(
            num_scalar_prefetch=1,
            grid=(length // tile,),
            in_specs=[
                row(inner), row(inner), row(STATE_DIM), row(LANES),
                fixed(ends.shape), fixed(coef.shape), fixed(initial.shape), fixed((1, inner)),
            ],
            out_specs=row(inner),
            scratch_shapes=[
                pltpu.VMEM((STATE_DIM, inner), jnp.bfloat16),
                pltpu.VMEM((LANES, inner), jnp.bfloat16),
                pltpu.VMEM((tile, inner), jnp.float32),
            ],
        ),
        out_shape=jax.ShapeDtypeStruct((length, inner), jnp.bfloat16),
        compiler_params=pltpu.CompilerParams(dimension_semantics=("arbitrary",)),
        cost_estimate=pl.CostEstimate(
            flops=40 * length * inner * STATE_DIM // 8, bytes_accessed=6 * length * inner, transcendentals=length * inner
        ),
        name="finish",
    )(nv, part, gate, read, ecum, ends, coef, initial, norm)


def pack_kernel(keep_ref, state_ref, out_ref):
    keep = keep_ref[pl.program_id(0)].astype(jnp.float32)
    peers, _, rows, _ = out_ref.shape
    for i in range(peers):
        out_ref[i, 0] = (state_ref[0, i * rows : (i + 1) * rows] * keep).astype(out_ref.dtype)


def pack_pieces(states, keep, peers):
    slots, rows, lanes = states.shape
    piece = rows // peers
    return pl.pallas_call(
        pack_kernel,
        grid_spec=pltpu.PrefetchScalarGridSpec(
            num_scalar_prefetch=1,
            grid=(slots,),
            in_specs=[pl.BlockSpec((1, rows, lanes), lambda i, keep: (i, 0, 0))],
            out_specs=pl.BlockSpec((peers, 1, piece, lanes), lambda i, keep: (0, i, 0, 0)),
        ),
        out_shape=jax.ShapeDtypeStruct((peers, slots, piece, lanes), jnp.bfloat16),
        compiler_params=pltpu.CompilerParams(dimension_semantics=("arbitrary",)),
        cost_estimate=pl.CostEstimate(flops=slots * rows * lanes, bytes_accessed=6 * slots * rows * lanes, transcendentals=0),
        name="pack",
    )(keep, states)


def route_kernel(slots, source_ref, got_ref, first_ref, rest_ref):
    peers = first_ref.shape[0]

    def one_peer(d, carry):
        first_ref[d, 0] = got_ref[source_ref[d * slots]]
        for k in range(1, slots):
            rest_ref[d, k - 1] = got_ref[source_ref[d * slots + k]]
        return carry

    lax.fori_loop(0, peers, one_peer, 0)


def route(source, got, peers, slots):
    count, rows, lanes = got.shape
    return pl.pallas_call(
        functools.partial(route_kernel, slots),
        grid_spec=pltpu.PrefetchScalarGridSpec(
            num_scalar_prefetch=1,
            grid=(1,),
            in_specs=[pl.BlockSpec(got.shape, lambda i, s: (0, 0, 0))],
            out_specs=[
                pl.BlockSpec((peers, 1, rows, lanes), lambda i, s: (0, 0, 0, 0)),
                pl.BlockSpec((peers, slots - 1, rows, lanes), lambda i, s: (0, 0, 0, 0)),
            ],
        ),
        out_shape=[
            jax.ShapeDtypeStruct((peers, 1, rows, lanes), got.dtype),
            jax.ShapeDtypeStruct((peers, slots - 1, rows, lanes), got.dtype),
        ],
        compiler_params=pltpu.CompilerParams(dimension_semantics=("arbitrary",)),
        cost_estimate=pl.CostEstimate(flops=count * rows * lanes, bytes_accessed=4 * count * rows * lanes, transcendentals=0),
        name="route",
    )(source, got)


def place_kernel(final_ref, got_ref, out_ref):
    slot = pl.program_id(0)
    peers, _, rows, _ = got_ref.shape

    @pl.when(slot == 0)
    def _():
        out_ref[...] = final_ref[...]

    @pl.when(slot > 0)
    def _():
        for i in range(peers):
            out_ref[0, i * rows : (i + 1) * rows] = got_ref[i, 0].astype(out_ref.dtype)


def place(final, got):
    peers, rest, rows, lanes = got.shape
    slots = rest + 1
    return pl.pallas_call(
        place_kernel,
        grid=(slots,),
        in_specs=[
            pl.BlockSpec((1, peers * rows, lanes), lambda i: (0, 0, 0)),
            pl.BlockSpec((peers, 1, rows, lanes), lambda i: (0, jnp.maximum(i - 1, 0), 0, 0)),
        ],
        out_specs=pl.BlockSpec((1, peers * rows, lanes), lambda i: (i, 0, 0)),
        out_shape=jax.ShapeDtypeStruct((slots, peers * rows, lanes), jnp.float32),
        compiler_params=pltpu.CompilerParams(dimension_semantics=("arbitrary",)),
        cost_estimate=pl.CostEstimate(
            flops=slots * peers * rows * lanes, bytes_accessed=6 * slots * peers * rows * lanes, transcendentals=0
        ),
        name="place",
    )(final, got)


def exchange(source):
    return lax.all_to_all(source, "req", split_axis=0, concat_axis=0, tiled=True)


def on_device(
    pool_states, inner_window, state_window, move_plan, active_mask, inputs_inner, inputs_state, gate_rows, step_raw,
    lengths, conv_weight, conv_bias, step_bias, decay_log, skip_weight, norm_weight,
):
    peers, me = lax.axis_size("req"), lax.axis_index("req")
    chain, rank = lax.axis_size("seq"), lax.axis_index("seq")
    slots, heads_own = pool_states.shape[:2]
    length, inner = inputs_inner.shape[1:]
    own_width = inner_window.shape[2]
    states = pool_states.reshape(slots, -1, pool_states.shape[-1])
    rows = states.shape[1]

    got = exchange(pack_pieces(states, active_mask, peers))
    got = got.reshape((peers * slots,) + got.shape[2:])

    every_plan = lax.all_gather(move_plan, "req").reshape(-1, 2)
    target = every_plan[:, 0] * slots + every_plan[:, 1]
    order = jnp.arange(peers * slots, dtype=jnp.int32)
    source = jnp.sum(jnp.where(target[None, :] == order[:, None], order[None, :], 0), axis=1).astype(jnp.int32)

    windows = jnp.concatenate([inner_window, state_window], axis=2)
    windows = jnp.where(active_mask[:, None, None] != 0, windows, jnp.zeros_like(windows))
    every_window = lax.all_gather(windows.reshape(slots, -1), "req", axis=0, tiled=True)
    own_source = lax.dynamic_slice_in_dim(source, me * slots, slots)
    moved_windows = jnp.take(every_window, own_source, axis=0).reshape(windows.shape)

    x, xs = inputs_inner[0], inputs_state[0]
    taps = KERNEL - 1
    tail = jnp.concatenate([x[length - taps :], xs[length - taps :]], axis=1)
    position = lengths[0] - taps + jnp.arange(taps, dtype=jnp.int32) - rank * length
    inside = (position >= 0) & (position < length)
    clipped = jnp.clip(position, 0, length - 1)
    last = jnp.concatenate([jnp.take(x, clipped, axis=0), jnp.take(xs, clipped, axis=0)], axis=1)
    last = jnp.where(inside[:, None], last, jnp.zeros_like(last))
    edges = lax.all_gather(jnp.concatenate([tail, last], axis=0), "seq")
    head = lax.all_gather(moved_windows[0], "seq")
    head_inner = jnp.moveaxis(head[:, :, :own_width], 0, 1).reshape(taps, -1)
    head_outer = jnp.moveaxis(head[:, :, own_width:], 0, 1).reshape(taps, -1)
    before = lax.dynamic_index_in_dim(edges[:, :taps], lax.rem(rank + chain - 1, chain), 0, keepdims=False)
    window = jnp.where(rank == 0, jnp.concatenate([head_inner, head_outer], axis=1), before)
    window = jnp.pad(window.astype(jnp.float32), ((HALO - taps, 0), (0, 0)))
    kept = jnp.sum(edges[:, taps:].astype(jnp.float32), axis=0).astype(jnp.bfloat16)
    outer_own = state_window.shape[2]
    kept_inner = lax.dynamic_slice_in_dim(kept, rank * own_width, own_width, 1)
    kept_outer = lax.dynamic_slice_in_dim(kept, inner + rank * outer_own, outer_own, 1)
    new_inner = jnp.concatenate([kept_inner[None], moved_windows[1:, :, :own_width]], axis=0)
    new_outer = jnp.concatenate([kept_outer[None], moved_windows[1:, :, own_width:]], axis=0)

    valid_count = (lengths - rank * length).astype(jnp.int32)
    skip_row = jnp.repeat(skip_weight, HEAD_DIM)[None]
    part, end, ecum, read = mix(
        valid_count, x, xs, window, conv_weight, conv_bias, step_raw[0], step_bias, decay_log, skip_row
    )
    heads = decay_log.shape[0]
    ends = lax.all_gather(end, "seq")
    decays = lax.all_gather(ecum[length - 1, :heads], "seq")

    index = jnp.arange(chain)
    between = (index[None, :, None] > index[:, None, None]) & (index[None, :, None] < rank)
    coef = jnp.prod(jnp.where(between, decays[None], 1.0), axis=1) * (index[:, None] < rank)
    prior_decay = jnp.prod(jnp.where(index[:, None] < rank, decays, 1.0), axis=0)
    coef = jnp.concatenate([coef, prior_decay[None]], axis=0)
    coef_row = jnp.repeat(coef, HEAD_DIM, axis=1)
    after = index[None, :, None] > index[:, None, None]
    suffix = jnp.prod(jnp.where(after, decays[None], 1.0), axis=1)
    suffix = jnp.concatenate([suffix, jnp.prod(decays, axis=0)[None]], axis=0)
    suffix_own = jnp.repeat(lax.dynamic_slice_in_dim(suffix, rank * heads_own, heads_own, 1), HEAD_DIM, axis=1)

    send_first, send_rest = route(source, got, peers, slots)
    initial_own = exchange(send_first).reshape(rows, -1)
    rest = exchange(send_rest)
    initial = lax.all_gather(initial_own, "seq", axis=0, tiled=True)
    out = finish(valid_count, part, gate_rows[0], read, ecum, ends, coef_row, initial, norm_weight[None])

    ends_own = lax.dynamic_slice_in_dim(ends, rank * own_width, own_width, 2).astype(jnp.float32)
    final = jnp.sum(ends_own * suffix_own[:chain, None, :], axis=0).T
    final = final + suffix_own[chain][:, None] * initial_own.astype(jnp.float32)
    new_states = place(final[None], rest).reshape(pool_states.shape)
    return (new_states, new_inner, new_outer, out[None])


def solution(mesh):
    return jax.shard_map(
        on_device,
        mesh=mesh,
        in_specs=(
            P("req", "seq", None, None), P("req", None, "seq"), P("req", None, "seq"), P("req", None), P("req"),
            P("req", "seq", None), P("req", "seq", None), P("req", "seq", None), P("req", "seq", None), P("req"),
            P(), P(), P(), P(), P(), P(),
        ),
        out_specs=(
            P("req", "seq", None, None), P("req", None, "seq"), P("req", None, "seq"), P("req", "seq", None),
        ),
        check_vma=False,
    )
```

time: 364 us -> 321 us (0.88)
  blocking collectives: 38.7 us -> 143 us
  waiting for transfers between devices: 86.7 us -> 25.5 us
  local copies, waits for them, and re-layouts: 83.9 us -> 36 us
  other arithmetic: 62.1 us -> 16.9 us
  Pallas kernels: 30.7 us -> 71.1 us
  matrix products: 25.2 us -> 0 us
  starting transfers between devices: 17.8 us -> 11.3 us
    all_gather x3 -> x5, blocking collectives: 33.1 us -> 129 us  [the longest x1 65 us: on_device(): every_plan = lax.all_gather(move_plan, 'req').reshape(-1, 2)]
    pallas_call x3 -> x5, Pallas kernels: 30.7 us -> 71.1 us  [the longest x1 25.1 us: mix(): pl.pallas_call(mix_kernel, grid_spec=pltpu.PrefetchScalarGridSpec(num_sca...]
    all_to_all x3 -> x2, waiting for transfers between devices: 59.8 us -> 19.9 us  [exchange(): lax.all_to_all(source, 'req', split_axis=0, concat_axis=0, tiled=True)]
    reshape x4 -> x2, local copies, waits for them, and re-layouts: 31.2 us -> 1.75 us  [the longest x1 1.67 us: on_device(): coef_row = jnp.repeat(coef, HEAD_DIM, axis=1)]
    dot_general x8 -> x0, matrix products: 25.2 us -> none  [the longest x2 15.9 us: block_local(): jnp.einsum('hts,shp->thp', weights, value_rows, preferred_element_type=jn...]
    all_gather x2, waiting for transfers between devices: 26.5 us -> 5.52 us  [the longest x1 5.52 us: on_device(): initial = lax.all_gather(initial_own, 'seq', axis=0, tiled=True)]
    add x7 -> x1, other arithmetic: 18.3 us -> 0.01 us  [on_device(): target = every_plan[:, 0] * slots + every_plan[:, 1]]
    while x19 -> x0, local copies, waits for them, and re-layouts: 14.6 us -> none  [the longest x2 10.6 us: local_parts(): lax.map(one_item, (to_items(value_rows), to_items(write_rows), to_items(r...]
  transfers between devices with their start and end apart: 9 -> 4, of which waited for: 4 -> 2; matrix products, arithmetic and copies ran while one was open for 44% -> 15% of each run, Pallas kernels for 6% -> 16%
where the time goes in v1:
time: 321 us; the launch traced here: 319 us
  blocking collectives  143 us (45%)
  Pallas kernels  71.1 us (22%)
  local copies, waits for them, and re-layouts  36 us (11%)
  waiting for transfers between devices  25.5 us (8%)
  other arithmetic  16.9 us (5%)
  between operations  14.9 us (5%)
  starting transfers between devices  11.3 us (4%)
    all_gather x1, blocking collectives, on_device(): every_plan = lax.all_gather(move_plan, 'req').reshape(-1, 2)  65 us
    all_gather x1, blocking collectives, on_device(): lax.all_gather(windows.reshape(slots, -1), 'req', axis=0, tiled=True)  47.6 us
    pallas_call x1, Pallas kernels, mix(): pl.pallas_call(mix_kernel, grid_spec=pltpu.PrefetchScalarGridSpec(num_sca...  25.1 us
    pallas_call x1, Pallas kernels, finish(): pl.pallas_call(finish_kernel, grid_spec=pltpu.PrefetchScalarGridSpec(num_...  22.3 us
    all_to_all x2, waiting for transfers between devices, exchange(): lax.all_to_all(source, 'req', split_axis=0, concat_axis=0, tiled=True)  19.9 us
    all_to_all x1, blocking collectives, exchange(): lax.all_to_all(source, 'req', split_axis=0, concat_axis=0, tiled=True)  13.9 us
    all_to_all x2, starting transfers between devices, exchange(): lax.all_to_all(source, 'req', split_axis=0, concat_axis=0, tiled=True)  11.2 us
    pallas_call x1, Pallas kernels, pack_pieces(): pl.pallas_call(pack_kernel, grid_spec=pltpu.PrefetchScalarGridSpec(num_sc...  9.87 us
  transfers between devices with their start and end apart: 4, of which 2 were waited for; matrix products, arithmetic and copies ran while one was open for 15% of the time, Pallas kernels for 16%

profile of v1, /device:TPU:0, one launch (start us, length us, event | category | flops | bytes accessed | tf_op | source)
XLA Modules:
  0.0 318.6 jit_solution(11274312959625219640)
XLA Ops:
  7.2 9.9 %pack.1 = bf16[8,13,128,128]{3,2,1,0:T(8,128)(2,1)} custom-call(s32[13]{0:T(128)} %keep_ref.1, f32[13,1024,128]{2,1,0:T(8,128)} %bitcast.61), custom_call_target="tpu_custom_call" | custom-call | flops 1703936 | bytes 10223616 | tf_op jit(solution)/shard_map/pack/pallas_call | solution.py:273
  17.1 7.4 %all-to-all-start = ((bf16[8,13,128,128]{3,2,1,0:T(8,128)(2,1)}), bf16[8,13,128,128]{3,2,1,0:T(8,128)(2,1)S(1)}, u32[]{:S(2)}, u32[]{:S(2)}) async-start(bf16[8,13,128,128]{3,2,1,0:T(8,128)(2,1)} %pack.1), calls=%async_computation | async-start | bytes 6815744 | tf_op jit(solution)/shard_map/all_to_all | solution.py:358
  27.4 1.3 slice.90.cws_ref
  28.7 1.5 slice.87.cw_ref
  30.2 65.0 %all-gather.3 = s32[8,13,2]{1,2,0:T(2,128)S(1)} all-gather(s32[1,13,2]{1,2,0:T(2,128)S(1)} %bitcast.81), channel_id=2, replica_groups=mesh['req'=8,'seq'=4] {'req'}, dimensions={0}, use_global_device_ids=true | all-gather | bytes 936 | tf_op jit(solution)/shard_map/all_gather | solution.py:376
  96.1 0.8 concatenate.30
  96.9 1.0 select_bitcast_fusion
  97.9 47.6 %all-gather.4 = bf16[8,13,3264]{2,1,0:T(8,128)(2,1)} all-gather(bf16[1,13,3264]{2,1,0:T(8,128)(2,1)S(1)} %select_bitcast_fusion), channel_id=1, replica_groups=mesh['req'=8,'seq'=4] {'req'}, dimensions={0}, use_global_device_ids=true | all-gather | bytes 763776 | tf_op jit(solution)/shard_map/all_gather | solution.py:383
  145.5 2.4 reshape.202
  147.8 1.9 gather_fusion
  149.9 5.2 %all_gather.33 = bf16[4,3,1088]{2,1,0:T(4,128)(2,1)S(1)} all-gather(bf16[1,3,1088]{2,1,0:T(4,128)(2,1)S(1)} %slice.78), channel_id=1, replica_groups=mesh['req'=8,'seq'=4] {'seq'}, dimensions={0}, use_global_device_ids=true | all-gather | bytes 32640 | tf_op jit(solution)/shard_map/all_gather | solution.py:396
  156.4 1.5 slice_bitcast_fusion
  157.9 2.1 gather_fusion.2
  160.0 3.5 %gather_fusion.1 = bf16[3,4096]{1,0:T(4,128)(2,1)S(1)} fusion(bf16[512,4096]{1,0:T(8,128)(2,1)} %bitcast.72, s32[1024]{0:T(1024)} %copy-done.8), kind=kCustom, calls=%fused_computation.1 | custom fusion | bytes 49164 | tf_op jit(solution)/shard_map/jit(_take)/gather | solution.py:393
  163.5 1.3 broadcast_select_fusion.3
  164.8 1.3 broadcast_select_fusion.1
  166.1 0.7 broadcast_in_dim.186
  167.6 1.0 copy.39
  168.6 0.8 maximum_select_fusion.1
  169.5 0.8 maximum_bitcast_fusion
  170.3 5.9 %all-gather.5 = bf16[4,6,4352]{2,1,0:T(8,128)(2,1)S(1)} all-gather(bf16[1,6,4352]{2,1,0:T(8,128)(2,1)S(1)} %maximum_bitcast_fusion), channel_id=3, replica_groups=mesh['req'=8,'seq'=4] {'seq'}, dimensions={0}, use_global_device_ids=true | all-gather | bytes 261120 | tf_op jit(solution)/shard_map/all_gather | solution.py:395
  176.2 0.7 slice_reduce_fusion
  176.9 0.8 maximum_select_fusion
  178.4 1.2 pad_bitcast_fusion
  180.2 0.8 pad_convert_fusion.step_ref
  180.9 25.1 %mix.1 = (bf16[512,4096]{1,0:T(8,128)(2,1)}, bf16[128,4096]{1,0:T(8,128)(2,1)}, f32[512,128]{1,0:T(8,128)}, bf16[512,128]{1,0:T(8,128)(2,1)}) custom-call(s32[1]{0:T(128)S(6)} %sub.37.nv_ref, bf16[512,4096]{1,0:T(8,128)(2,1)} %bitcast.73, f32[8,4096]{1,0:T(8,128)} %slice.110.win_ref, f32[4,4096]{1,0:T(4,128)} %slice.87.cw_ref, f32[1,4096]{1,0:T(1,128)} %bitcast.75, ...), custom_call_target="tpu_custom_call" | custom-call | flops 17179869184 | bytes 8388608 | tf_op jit(solution)/shard_map/mix/pallas_call | solution.py:132
  206.1 1.7 copy-done
  207.9 4.6 %route.1 = (bf16[8,1,128,128]{3,2,1,0:T(8,128)(2,1)}, bf16[8,12,128,128]{3,2,1,0:T(8,128)(2,1)}) custom-call(s32[104]{0:T(128)} %copy-done.11, bf16[104,128,128]{2,1,0:T(8,128)(2,1)} %bitcast.60), custom_call_target="tpu_custom_call" | custom-call | flops 1703936 | bytes 6815744 | tf_op jit(solution)/shard_map/route/pallas_call | solution.py:302
  212.5 13.9 %all_to_all.15 = bf16[8,1,128,128]{3,2,1,0:T(8,128)(2,1)} all-to-all(bf16[8,1,128,128]{3,2,1,0:T(8,128)(2,1)} %get-tuple-element.12), channel_id=1, replica_groups=mesh['req'=8,'seq'=4] {'req'}, dimensions={0} | all-to-all | bytes 524288 | tf_op jit(solution)/shard_map/all_to_all | solution.py:358
  226.4 3.8 %all-to-all-start.2 = ((bf16[8,12,128,128]{3,2,1,0:T(8,128)(2,1)}), bf16[8,12,128,128]{3,2,1,0:T(8,128)(2,1)S(1)}, u32[]{:S(2)}, u32[]{:S(2)}) async-start(bf16[8,12,128,128]{3,2,1,0:T(8,128)(2,1)} %get-tuple-element.13), calls=%async_computation.2 | async-start | bytes 6291456 | tf_op jit(solution)/shard_map/all_to_all | solution.py:358
  230.2 0.8 gather.17
  231.1 1.0 broadcast_select_fusion
  232.8 0.7 fusion.2
  233.5 0.7 dynamic-slice_bitcast_fusion
  234.2 1.0 pad_maximum_fusion.1
  235.2 1.2 slice_bitcast_fusion.4
  237.7 5.2 %all-gather.6 = f32[4,1,64]{2,1,0:T(1,128)S(1)} all-gather(f32[1,1,64]{2,1,0:T(1,128)} %slice_bitcast_fusion.4), channel_id=1, replica_groups=mesh['req'=8,'seq'=4] {'seq'}, dimensions={0}, use_global_device_ids=true | all-gather | bytes 1280 | tf_op jit(solution)/shard_map/all_gather | solution.py:416
  243.4 0.8 select_reduce_fusion.3
  244.3 0.8 broadcast_in_dim.206
  245.0 1.7 reshape.169.coef_ref
  246.7 2.3 multiply_reduce_fusion
  249.0 2.1 copy.40
  251.1 2.0 fusion.final_ref
  253.1 5.5 %all-gather.10.cloned.1.call-done.init_ref = bf16[4096,128]{1,0:T(8,128)(2,1)} async-done(((bf16[1024,128]{1,0:T(8,128)(2,1)}), bf16[4096,128]{1,0:T(8,128)(2,1)}) %all-gather.10.cloned.1.call-update) | async-done | bytes 1048592 | tf_op jit(solution)/shard_map/all_gather | solution.py:432
  258.7 22.3 %finish.1 = bf16[512,4096]{1,0:T(8,128)(2,1)} custom-call(s32[1]{0:T(128)S(6)} %sub.37.nv_ref, bf16[512,4096]{1,0:T(8,128)(2,1)} %get-tuple-element.14.part_ref, bf16[512,4096]{1,0:T(8,128)(2,1)} %bitcast.65, bf16[512,128]{1,0:T(8,128)(2,1)} %get-tuple-element.15.read_ref, f32[512,128]{1,0:T(8,128)} %get-tuple-element.11.ecum_ref, ...), custom_call_target="tpu_custom_call" | custom-call | flops 1342177280 | bytes 12582912 | tf_op jit(solution)/shard_map/finish/pallas_call | solution.py:238
  281.0 19.9 %all-to-all-done.2.got_ref = bf16[8,12,128,128]{3,2,1,0:T(8,128)(2,1)S(1)} async-done(((bf16[8,12,128,128]{3,2,1,0:T(8,128)(2,1)}), bf16[8,12,128,128]{3,2,1,0:T(8,128)(2,1)S(1)}, u32[]{:S(2)}, u32[]{:S(2)}) %all-to-all-start.2) | async-done | bytes 3145760 | tf_op jit(solution)/shard_map/all_to_all | solution.py:358
  300.9 1.6 copy-done.1
  302.5 9.2 %place.1 = f32[13,1024,128]{2,1,0:T(8,128)} custom-call(f32[1,1024,128]{2,1,0:T(8,128)} %fusion.final_ref, bf16[8,12,128,128]{3,2,1,0:T(8,128)(2,1)} %copy-done.1), custom_call_target="tpu_custom_call" | custom-call | flops 1703936 | bytes 10223616 | tf_op jit(solution)/shard_map/place/pallas_call | solution.py:340
  (81 shorter events, 9.4 us)
Async XLA Ops:
  17.0 7.5 %copy-start.13 = (s32[13]{0:T(128)S(1)}, s32[13]{0:T(128)}, u32[]{:S(2)}) copy-start(s32[13]{0:T(128)} %keep_ref.1) | copy-start | bytes 160
  17.0 9.3 %copy-start.6 = (f32[4352]{0:T(1024)S(1)}, f32[4352]{0:T(1024)}, u32[]{:S(2)}) copy-start(f32[4352]{0:T(1024)} %param.27) | copy-start | bytes 52228
  17.0 13.2 %copy-start.12 = (s32[13,2]{0,1:T(2,128)S(1)}, s32[13,2]{0,1:T(2,128)}, u32[]{:S(2)}) copy-start(s32[13,2]{0,1:T(2,128)} %param.19) | copy-start | bytes 316
  17.0 78.9 %copy-start.5 = (bf16[13,3,1024]{2,0,1:T(8,128)(2,1)S(1)}, bf16[13,3,1024]{2,0,1:T(8,128)(2,1)}, u32[]{:S(2)}) copy-start(bf16[13,3,1024]{2,0,1:T(8,128)(2,1)} %param.17) | copy-start | bytes 239620
  17.0 78.9 %copy-start.7 = (bf16[13,3,64]{2,0,1:T(8,128)(2,1)S(1)}, bf16[13,3,64]{2,0,1:T(8,128)(2,1)}, u32[]{:S(2)}) copy-start(bf16[13,3,64]{2,0,1:T(8,128)(2,1)} %param.18) | copy-start | bytes 14980
  17.1 189.1 %all-to-all-start = ((bf16[8,13,128,128]{3,2,1,0:T(8,128)(2,1)}), bf16[8,13,128,128]{3,2,1,0:T(8,128)(2,1)S(1)}, u32[]{:S(2)}, u32[]{:S(2)}) async-start(bf16[8,13,128,128]{3,2,1,0:T(8,128)(2,1)} %pack.1), calls=%async_computation | async-start | bytes 6815744 | tf_op jit(solution)/shard_map/all_to_all | solution.py:358
  24.5 222.2 %all-gather.12.cloned.1.call-start = ((), (), s32[]{:S(2)}) async-start(), calls=%async_computation.4 | async-start | bytes 5242880 | tf_op jit(solution)/shard_map/all_gather | solution.py:415
  95.4 0.5 copy-start.11
  95.9 64.1 %copy-start.9 = (pred[13]{0:T(512)(128)(4,1)}, pred[13]{0:T(512)(128)(4,1)S(1)}, u32[]{:S(2)}) copy-start(pred[13]{0:T(512)(128)(4,1)S(1)} %get-tuple-element.30) | copy-start | bytes 43
  96.0 60.4 %copy-start.14 = (s32[3]{0:T(128)S(1)}, s32[3]{0:T(128)}, u32[]{:S(2)}) copy-start(s32[3]{0:T(128)} %fusion.3) | copy-start | bytes 40
  149.7 17.2 %copy-start.3 = (bf16[13,3264]{1,0:T(8,128)(2,1)}, bf16[13,3264]{1,0:T(8,128)(2,1)S(1)}, u32[]{:S(2)}) copy-start(bf16[13,3264]{1,0:T(8,128)(2,1)S(1)} %gather_fusion) | copy-start | bytes 254596
  156.4 3.6 %copy-start.8 = (s32[1024]{0:T(1024)}, s32[1024]{0:T(1024)S(1)}, u32[]{:S(2)}) copy-start(s32[1024]{0:T(1024)S(1)} %pad_clamp_fusion) | copy-start | bytes 12292
  206.1 1.8 copy-start
  212.5 17.7 %copy-start.4 = (bf16[13,3264]{1,0:T(8,128)(2,1)S(1)}, bf16[13,3264]{1,0:T(8,128)(2,1)}, u32[]{:S(2)}) copy-start(bf16[13,3264]{1,0:T(8,128)(2,1)} %copy-done.3) | copy-start | bytes 254596
  212.5 18.5 %copy-start.10 = (pred[13]{0:T(512)(128)(4,1)S(1)}, pred[13]{0:T(512)(128)(4,1)}, u32[]{:S(2)}) copy-start(pred[13]{0:T(512)(128)(4,1)} %copy-done.9) | copy-start | bytes 43
  226.4 24.7 %copy-start.2 = (bf16[8,1,128,128]{3,2,1,0:T(8,128)(2,1)S(1)}, bf16[8,1,128,128]{3,2,1,0:T(8,128)(2,1)}, u32[]{:S(2)}) copy-start(bf16[8,1,128,128]{3,2,1,0:T(8,128)(2,1)} %all_to_all.15) | copy-start | bytes 786436
  226.4 74.5 %all-to-all-start.2 = ((bf16[8,12,128,128]{3,2,1,0:T(8,128)(2,1)}), bf16[8,12,128,128]{3,2,1,0:T(8,128)(2,1)S(1)}, u32[]{:S(2)}, u32[]{:S(2)}) async-start(bf16[8,12,128,128]{3,2,1,0:T(8,128)(2,1)} %get-tuple-element.13), calls=%async_computation.2 | async-start | bytes 6291456 | tf_op jit(solution)/shard_map/all_to_all | solution.py:358
  230.2 28.5 %all-gather.10.cloned.1.call-start = ((), (), s32[]{:S(2)}) async-start(), calls=%async_computation.3 | async-start | bytes 1310720 | tf_op jit(solution)/shard_map/all_gather | solution.py:432
  232.8 3.6 %copy-start.15 = (pred[4]{0:T(512)(128)(4,1)}, pred[4]{0:T(512)(128)(4,1)S(1)}, u32[]{:S(2)}) copy-start(pred[4]{0:T(512)(128)(4,1)S(1)} %get-tuple-element.34) | copy-start | bytes 16
  300.9 1.6 copy-start.1
Sparse Core Ops, SparseCore 0:
  206.2 34.0 all-gather.11
  241.9 16.6 all-gather.9
